TPU v7x, 16 devices: a whole 2x2x2 slice. The times are simulated.
16 devices in a mesh: data: 4 (over z, y), tp: 4 (over x, core).
Axes of the slice: x: 2, y: 2, z: 2, core: 2. Of those that a mesh axis runs over, the one named last changes fastest.
Arguments:
- x_all: bfloat16 [256, 2560], P(('data', 'tp')), parts along dimension 0
- ln_gammas: float32 [2, 2560], replicated
- w_in: bfloat16 [2, 2560, 10240], P(None, None, 'tp')
- w_out: bfloat16 [2, 10240, 2560], P(None, 'tp')
Outputs:
- output: bfloat16 [256, 2560], P(('data', 'tp')), parts along dimension 0
There are 4 independent parts. A program takes and returns all parts, laid end to end along the dimension named above; an argument that names none is the same for every part.
All inputs are finite; a program needn't handle non-finite values.
Results may differ from a plain program's by a relative error of at most 0.0100232.
Values are sent between devices in bfloat16 or wider.
A program may use at most 1 GiB of HBM per device.

v0:
```python
import jax
import jax.numpy as jnp
from jax import lax
from jax.sharding import PartitionSpec as P, NamedSharding

LN_EPS = 1e-6


def layer_norm(x_rows, gamma_row):
    x_f32 = x_rows.astype(jnp.float32)
    mean_val = jnp.mean(x_f32, axis=-1, keepdims=True)
    centered = x_f32 - mean_val
    var_val = jnp.mean(centered * centered, axis=-1, keepdims=True)
    return (centered * lax.rsqrt(var_val + LN_EPS) * gamma_row).astype(jnp.bfloat16)


def solution(mesh):
    def local_stack(x_local, ln_gammas, w_in, w_out):
        residual = x_local
        for layer_idx in range(w_in.shape[0]):
            normed = layer_norm(residual, ln_gammas[layer_idx])
            gathered = lax.all_gather(normed, 'tp', axis=0, tiled=True)
            hidden = jax.nn.gelu(jnp.dot(gathered, w_in[layer_idx], preferred_element_type=jnp.float32), approximate=True).astype(jnp.bfloat16)
            partial_out = jnp.dot(hidden, w_out[layer_idx], preferred_element_type=jnp.float32)
            reduced = lax.psum_scatter(partial_out, 'tp', scatter_dimension=0, tiled=True)
            residual = (residual.astype(jnp.float32) + reduced).astype(jnp.bfloat16)
        return residual

    return jax.shard_map(
        local_stack,
        mesh=mesh,
        in_specs=(P(('data', 'tp'), None), P(None, None), P(None, None, 'tp'), P(None, 'tp', None)),
        out_specs=P(('data', 'tp'), None),
        check_vma=False,
    )
```

profile of v0, /device:TPU:0, one launch (start us, length us, event | category | flops | bytes accessed | tf_op | source)
XLA Modules:
  0.0 96.6 jit_solution(8731403223755138552)
XLA Ops:
  6.5 0.0 copy-start
  6.5 0.0 reduce-scatter.3.cloned.1.call-start
  6.5 1.1 %convert_reduce_fusion.1 = f32[16]{0:T(128)S(1)} fusion(bf16[16,2560]{1,0:T(8,128)(2,1)} %param.4), kind=kLoop, calls=%fused_computation.43 | loop fusion | flops 81904 | bytes 81984 | tf_op jit(solution)/shard_map/reduce_sum | solution.py:11
  7.6 1.1 %fusion.55 = f32[16]{0:T(128)S(1)} fusion(bf16[16,2560]{1,0:T(8,128)(2,1)} %param.4, f32[16]{0:T(128)S(1)} %broadcast_multiply_fusion.1), kind=kLoop, calls=%fused_computation.51 | loop fusion | flops 163824 | bytes 82048 | tf_op jit(solution)/shard_map/reduce_sum | solution.py:13
  8.7 0.9 slice_reduce_fusion
  9.6 1.0 %fusion.57 = bf16[16,2560]{1,0:T(8,128)(2,1)S(1)} fusion(bf16[16,2560]{1,0:T(8,128)(2,1)} %param.4, f32[2560]{0:T(1024)S(1)} %get-tuple-element.6, f32[16]{0:T(128)S(1)} %add_rsqrt_fusion.1, f32[16]{0:T(128)S(1)} %broadcast_multiply_fusion.1), kind=kLoop, calls=%fused_computation.53 | loop fusion | flops 204800 | bytes 174208 | tf_op jit(solution)/shard_map/convert_element_type | solution.py:14
  10.6 7.8 %all_gather.6 = bf16[64,2560]{1,0:T(8,128)(2,1)S(1)} all-gather(bf16[16,2560]{1,0:T(8,128)(2,1)S(1)} %fusion.57), channel_id=1, replica_groups=mesh['data'=4,'tp'=4] {'tp'}, dimensions={0}, use_global_device_ids=true | all-gather | bytes 409600 | tf_op jit(solution)/shard_map/all_gather | solution.py:22
  18.4 11.9 %fusion.4 = f32[64,2560]{1,0:T(8,128)} fusion(bf16[2,2560,2560]{2,1,0:T(8,128)(2,1)} %param.7, bf16[64,2560]{1,0:T(8,128)(2,1)S(1)} %all_gather.6, bf16[2,2560,2560]{2,1,0:T(8,128)(2,1)} %param.6), kind=kOutput, calls=%fused_computation.4 | convolution fusion | flops 1679196160 | bytes 27197440 | tf_op jit(solution)/shard_map/dot_general | solution.py:24
  30.3 0.0 reduce-scatter.3.cloned.1.call-update
  30.4 0.0 reduce-scatter.5.cloned.1.call-start
  30.4 19.6 %reduce-scatter.3.cloned.1.call-done = f32[16,2560]{1,0:T(8,128)} async-done(((f32[64,2560]{1,0:T(8,128)}), f32[16,2560]{1,0:T(8,128)}) %reduce-scatter.3.cloned.1.call-update) | async-done | bytes 163856 | tf_op jit(solution)/shard_map/reduce_scatter | solution.py:25
  50.0 0.0 copy-done
  50.0 1.0 %convert_reduce_fusion = (f32[16]{0:T(128)S(1)}, bf16[16,2560]{1,0:T(8,128)(2,1)S(1)}) fusion(f32[16,2560]{1,0:T(8,128)} %reduce-scatter.3.cloned.1.call-done, bf16[16,2560]{1,0:T(8,128)(2,1)S(1)} %copy-done), kind=kLoop, calls=%fused_computation.40 | loop fusion | flops 204784 | bytes 327744 | tf_op jit(solution)/shard_map/reduce_sum | solution.py:11
  51.1 0.2 fusion.52
  51.3 0.1 fusion.54
  51.4 6.0 %all_gather.7 = bf16[64,2560]{1,0:T(8,128)(2,1)S(1)} all-gather(bf16[16,2560]{1,0:T(8,128)(2,1)S(1)} %fusion.54), channel_id=1, replica_groups=mesh['data'=4,'tp'=4] {'tp'}, dimensions={0}, use_global_device_ids=true | all-gather | bytes 409600 | tf_op jit(solution)/shard_map/all_gather | solution.py:22
  57.4 11.9 %fusion = f32[64,2560]{1,0:T(8,128)} fusion(bf16[2,2560,2560]{2,1,0:T(8,128)(2,1)} %param.7, bf16[64,2560]{1,0:T(8,128)(2,1)S(1)} %all_gather.7, bf16[2,2560,2560]{2,1,0:T(8,128)(2,1)} %param.6), kind=kOutput, calls=%fused_computation | convolution fusion | flops 1679196160 | bytes 27197440 | tf_op jit(solution)/shard_map/dot_general | solution.py:24
  69.3 0.0 reduce-scatter.5.cloned.1.call-update
  69.3 18.8 %reduce-scatter.5.cloned.1.call-done = f32[16,2560]{1,0:T(8,128)} async-done(((f32[64,2560]{1,0:T(8,128)}), f32[16,2560]{1,0:T(8,128)}) %reduce-scatter.5.cloned.1.call-update) | async-done | bytes 163856 | tf_op jit(solution)/shard_map/reduce_scatter | solution.py:25
  88.2 1.6 %fusion.59 = bf16[16,2560]{1,0:T(8,128)(2,1)} fusion(f32[16,2560]{1,0:T(8,128)} %reduce-scatter.5.cloned.1.call-done, bf16[16,2560]{1,0:T(8,128)(2,1)S(1)} %get-tuple-element.8), kind=kLoop, calls=%fused_computation.55 | loop fusion | flops 122880 | bytes 327680 | tf_op jit(solution)/shard_map/convert_element_type | solution.py:26
  (4 shorter events, 0.0 us)
Async XLA Ops:
  6.5 43.5 %copy-start = (bf16[16,2560]{1,0:T(8,128)(2,1)S(1)}, bf16[16,2560]{1,0:T(8,128)(2,1)}, u32[]{:S(2)}) copy-start(bf16[16,2560]{1,0:T(8,128)(2,1)} %param.4) | copy-start | bytes 245764
  6.5 43.5 %reduce-scatter.3.cloned.1.call-start = ((), (), s32[]{:S(2)}) async-start(), calls=%async_computation.2 | async-start | bytes 819200 | tf_op jit(solution)/shard_map/reduce_scatter | solution.py:25
  30.4 57.8 %reduce-scatter.5.cloned.1.call-start = ((), (), s32[]{:S(2)}) async-start(), calls=%async_computation.3 | async-start | bytes 819200 | tf_op jit(solution)/shard_map/reduce_scatter | solution.py:25
Sparse Core Ops, SparseCore 0:
  30.5 19.5 reduce-scatter.2
  69.4 18.6 reduce-scatter.4
where the time goes:
time: 96.9 us; the launch traced here: 96.6 us
  waiting for transfers between devices  38.5 us (40%)
  matrix products  23.8 us (25%)
  blocking collectives  13.8 us (14%)
  between operations  13.4 us (14%)
  other arithmetic  6.11 us (6%)
    reduce_scatter x2, waiting for transfers between devices, local_stack(): lax.psum_scatter(partial_out, 'tp', scatter_dimension=0, tiled=True)  38.4 us
    dot_general x2, matrix products, local_stack(): jnp.dot(hidden, w_out[layer_idx], preferred_element_type=jnp.float32)  23.8 us
    all_gather x2, blocking collectives, local_stack(): gathered = lax.all_gather(normed, 'tp', axis=0, tiled=True)  13.8 us
    reduce_sum x2, other arithmetic, layer_norm(): mean_val = jnp.mean(x_f32, axis=-1, keepdims=True)  2.13 us
  transfers between devices with their start and end apart: 2, of which 2 were waited for; matrix products, arithmetic and copies ran while one was open for 0% of the time, Pallas kernels for 0%

commit v1 on v0

v1 whole, which is shorter than its diff:
```python
import functools
import jax
import jax.numpy as jnp
from jax import lax
from jax.experimental import pallas as pl
from jax.experimental.pallas import tpu as pltpu
from jax.sharding import PartitionSpec as P

LN_EPS = 1e-6
MESH = pl.DeviceIdType.MESH

BW1 = 512
BW2 = 256
GW = 1280
LAG_SUM = (1, 3)
LAG_OUT = (4, 10)
LAG_RELAY = (7, 10)


def normalize(rows_f32, gamma_row):
    mean_val = jnp.mean(rows_f32, axis=-1, keepdims=True)
    centered = rows_f32 - mean_val
    var_val = jnp.mean(centered * centered, axis=-1, keepdims=True)
    return (centered * lax.rsqrt(var_val + LN_EPS) * gamma_row).astype(jnp.bfloat16)


def kernel(x_hbm, gam_hbm, w_in, w_out, out_ref,
           wv, x_own, gam, xg, xn, h, part, part_in, sum_out, sum_in, yg,
           lsem, wsem1, wsem2, g_sem, d2d_sem, ici_sem, y_sem):
    n_layers, width, ff = w_in.shape
    n1, n2, ng = ff // BW1, width // BW2, width // GW
    me = lax.axis_index("tp")
    chip, core = lax.div(me, 2), lax.rem(me, 2)
    mate = {"tp": chip * 2 + (1 - core)}
    peer = {"tp": (1 - chip) * 2 + core}
    R = x_own.shape[0]
    mine = core * 2 + chip
    across = core * 2 + (1 - chip)

    def rows(block, n=1):
        return pl.ds(pl.multiple_of(block * R, R), n * R)

    load_x = pltpu.make_async_copy(x_hbm, x_own, lsem.at[0])
    load_g = pltpu.make_async_copy(gam_hbm, gam, lsem.at[1])
    load_x.start()
    load_g.start()
    loads1, loads2 = {}, {}
    for l in range(n_layers):
        for j in range(n1):
            cols = pl.ds(j * BW1, BW1)
            loads1[l, j] = pltpu.make_async_copy(
                w_in.at[l, :, cols], wv.at[2 * l, :, cols], wsem1.at[l, j])
            loads1[l, j].start()
        for j in range(n2):
            cols = pl.ds(j * BW2, BW2)
            loads2[l, j] = pltpu.make_async_copy(
                w_out.at[l, :, cols], wv.at[2 * l + 1, :, cols], wsem2.at[l, j])
            loads2[l, j].start()

    barrier = pltpu.get_barrier_semaphore()
    for other in (mate, peer):
        pl.semaphore_signal(barrier, inc=1, device_id=other, device_id_type=MESH)

    sends = []

    def remote(src, dst, sems, device, *idx):
        copy = pltpu.make_async_remote_copy(
            src_ref=src, dst_ref=dst, send_sem=sems.at[(0,) + idx], recv_sem=sems.at[(1,) + idx],
            device_id=device, device_id_type=MESH)
        return copy

    def launch(copy):
        copy.start()
        sends.append(copy)

    load_x.wait()
    load_g.wait()
    own = normalize(x_own[...].astype(jnp.float32), gam[0:1, :])
    for g in range(ng):
        xg[g, rows(mine), :] = own[:, g * GW:(g + 1) * GW]
    pl.semaphore_wait(barrier, 2)

    arrive = {}
    for g in range(ng):
        block = xg.at[g, rows(mine)]
        to_peer = remote(block, block, g_sem, peer, 0, g)
        launch(to_peer)
        to_mate = remote(block, block, g_sem, mate, 1, g)
        launch(to_mate)
        arrive[g] = (to_peer, to_mate)
    relays = []
    for g in range(ng):
        arrive[g][0].wait_recv()
        block = xg.at[g, rows(across)]
        relay = remote(block, block, g_sem, mate, 2, g)
        launch(relay)
        relays.append(relay)
    for g in range(ng):
        arrive[g][1].wait_recv()
        relays[g].wait_recv()
        xn[:, g * GW:(g + 1) * GW] = xg[g]

    for l in range(n_layers):
        last = l == n_layers - 1
        for j in range(n1):
            cols = pl.ds(j * BW1, BW1)
            loads1[l, j].wait()
            u = jnp.dot(xn[...], wv[2 * l, :, cols], preferred_element_type=jnp.float32)
            h[:, cols] = jax.nn.gelu(u, approximate=True).astype(jnp.bfloat16)

        d2d, ici, yq, ym, yr = {}, {}, {}, {}, {}
        for step in range(n2 + max(LAG_SUM[l], LAG_OUT[l], LAG_RELAY[l])):
            j = step
            if j < n2:
                cols = pl.ds(j * BW2, BW2)
                loads2[l, j].wait()
                part[l, j] = jnp.dot(h[...], wv[2 * l + 1, :, cols], preferred_element_type=jnp.float32)
                d2d[j] = remote(part.at[l, j, rows((1 - core) * 2, 2)], part_in.at[l, j],
                                d2d_sem, mate, l, j)
                launch(d2d[j])
            j = step - LAG_SUM[l]
            if 0 <= j < n2:
                d2d[j].wait_recv()
                sum_out[l, j] = part[l, j, rows(across), :] + part_in[l, j, rows(1 - chip), :]
                ici[j] = remote(sum_out.at[l, j], sum_in.at[l, j], ici_sem, peer, l, j)
                launch(ici[j])
            j = step - LAG_OUT[l]
            if 0 <= j < n2:
                cols = pl.ds(j * BW2, BW2)
                ici[j].wait_recv()
                total = part[l, j, rows(mine), :] + part_in[l, j, rows(chip), :] + sum_in[l, j]
                y = (x_own[:, cols].astype(jnp.float32) + total).astype(jnp.bfloat16)
                if last:
                    out_ref[:, cols] = y
                else:
                    x_own[:, cols] = y
                    yg[j, rows(mine), :] = y
                    block = yg.at[j, rows(mine)]
                    yq[j] = remote(block, block, y_sem, peer, 0, j)
                    launch(yq[j])
                    ym[j] = remote(block, block, y_sem, mate, 1, j)
                    launch(ym[j])
            j = step - LAG_RELAY[l]
            if not last and 0 <= j < n2:
                yq[j].wait_recv()
                block = yg.at[j, rows(across)]
                yr[j] = remote(block, block, y_sem, mate, 2, j)
                launch(yr[j])
        if not last:
            for j in range(n2):
                ym[j].wait_recv()
                yr[j].wait_recv()
            for b in range(4):
                r = slice(b * R, (b + 1) * R)
                full = jnp.concatenate([yg[j, r, :] for j in range(n2)], axis=1)
                xn[r, :] = normalize(full.astype(jnp.float32), gam[l + 1:l + 2, :])

    for copy in sends:
        copy.wait_send()


def solution(mesh):
    def local_stack(x_local, ln_gammas, w_in, w_out):
        R, width = x_local.shape
        n_layers, _, ff = w_in.shape
        S = 4 * R
        n1, n2, ng = ff // BW1, width // BW2, width // GW
        f32, bf16 = jnp.float32, jnp.bfloat16
        return pl.pallas_call(
            kernel,
            out_shape=jax.ShapeDtypeStruct((R, width), bf16),
            in_specs=[pl.BlockSpec(memory_space=pl.ANY)] * 4,
            out_specs=pl.BlockSpec(memory_space=pltpu.VMEM),
            scratch_shapes=[
                pltpu.VMEM((2 * n_layers, width, ff), bf16),
                pltpu.VMEM((R, width), bf16),
                pltpu.VMEM((n_layers, width), f32),
                pltpu.VMEM((ng, S, GW), bf16),
                pltpu.VMEM((S, width), bf16),
                pltpu.VMEM((S, ff), bf16),
                pltpu.VMEM((n_layers, n2, S, BW2), f32),
                pltpu.VMEM((n_layers, n2, 2 * R, BW2), f32),
                pltpu.VMEM((n_layers, n2, R, BW2), f32),
                pltpu.VMEM((n_layers, n2, R, BW2), f32),
                pltpu.VMEM((n2, S, BW2), bf16),
                pltpu.SemaphoreType.DMA((2,)),
                pltpu.SemaphoreType.DMA((n_layers, n1)),
                pltpu.SemaphoreType.DMA((n_layers, n2)),
                pltpu.SemaphoreType.DMA((2, 3, ng)),
                pltpu.SemaphoreType.DMA((2, n_layers, n2)),
                pltpu.SemaphoreType.DMA((2, n_layers, n2)),
                pltpu.SemaphoreType.DMA((2, 3, n2)),
            ],
            compiler_params=pltpu.CompilerParams(
                collective_id=0, has_side_effects=True, vmem_limit_bytes=66_000_000),
            name="mlp_stack",
        )(x_local, ln_gammas, w_in, w_out)

    return jax.shard_map(
        local_stack,
        mesh=mesh,
        in_specs=(P(('data', 'tp'), None), P(None, None), P(None, None, 'tp'), P(None, 'tp', None)),
        out_specs=P(('data', 'tp'), None),
        check_vma=False,
    )
```

time: 96.9 us -> 56.4 us (0.58)
  Pallas kernels: 0 us -> 54.8 us
  waiting for transfers between devices: 38.5 us -> 0 us
  matrix products: 23.8 us -> 0 us
  blocking collectives: 13.8 us -> 0 us
  between operations: 13.4 us -> 0.01 us
  other arithmetic: 6.11 us -> 0 us
    pallas_call x0 -> x1, Pallas kernels: none -> 54.8 us  [local_stack(): pl.pallas_call(kernel, out_shape=jax.ShapeDtypeStruct((R, width), bf16),...]
    reduce_scatter x2 -> x0, waiting for transfers between devices: 38.4 us -> none  [local_stack(): lax.psum_scatter(partial_out, 'tp', scatter_dimension=0, tiled=True)]
    dot_general x2 -> x0, matrix products: 23.8 us -> none  [local_stack(): jnp.dot(hidden, w_out[layer_idx], preferred_element_type=jnp.float32)]
    all_gather x2 -> x0, blocking collectives: 13.8 us -> none  [local_stack(): gathered = lax.all_gather(normed, 'tp', axis=0, tiled=True)]
    reduce_sum x4 -> x0, other arithmetic: 3.43 us -> none  [the longest x2 2.13 us: layer_norm(): mean_val = jnp.mean(x_f32, axis=-1, keepdims=True)]
    convert_element_type x3 -> x0, other arithmetic: 2.65 us -> none  [the longest x1 1.57 us: local_stack(): residual = (residual.astype(jnp.float32) + reduced).astype(jnp.bfloat16)]
    unnamed x2 -> x1, local copies, waits for them, and re-layouts: 0.01 us -> 1.53 us
  transfers between devices with their start and end apart: 2 -> 0, of which waited for: 2 -> 0; matrix products, arithmetic and copies ran while one was open for 0% -> 0% of each run, Pallas kernels for 0% -> 0%
where the time goes in v1:
time: 56.4 us; the launch traced here: 56.3 us
  Pallas kernels  54.8 us (97%)
  local copies, waits for them, and re-layouts  1.53 us (3%)
    pallas_call x1, Pallas kernels, local_stack(): pl.pallas_call(kernel, out_shape=jax.ShapeDtypeStruct((R, width), bf16),...  54.8 us
    unnamed x1, local copies, waits for them, and re-layouts  1.53 us

profile of v1, /device:TPU:0, one launch (start us, length us, event | category | flops | bytes accessed | tf_op | source)
XLA Modules:
  0.0 56.3 jit_solution(3989399498788294225)
XLA Ops:
  0.0 54.8 %mlp_stack.1 = bf16[16,2560]{1,0:T(8,128)(2,1)} custom-call(bf16[16,2560]{1,0:T(8,128)(2,1)} %x_hbm.1, f32[2,2560]{1,0:T(2,128)} %gam_hbm.1, bf16[2,2560,2560]{2,1,0:T(8,128)(2,1)} %w_in.1, bf16[2,2560,2560]{2,1,0:T(8,128)(2,1)} %w_out.1), custom_call_target="tpu_custom_call" | custom-call | tf_op jit(solution)/shard_map/mlp_stack/pallas_call | solution.py:169
  54.8 1.5 %copy.6 = bf16[16,2560]{1,0:T(8,128)(2,1)} copy(bf16[16,2560]{1,0:T(8,128)(2,1)} %mlp_stack.1) | data formatting | bytes 163840

commit v2 on v1

--- a/solution.py
+++ b/solution.py
@@ -10,11 +10,12 @@
 MESH = pl.DeviceIdType.MESH
 
 BW1 = 512
-BW2 = 256
+BW2 = 512
 GW = 1280
-LAG_SUM = (1, 3)
-LAG_OUT = (4, 10)
-LAG_RELAY = (7, 10)
+MXU_ROWS = 128
+LAG_SUM = (1, 2)
+LAG_OUT = (3, 5)
+LAG_RELAY = (5, 5)
 
 
 def normalize(rows_f32, gamma_row):
@@ -34,6 +35,9 @@
     mate = {"tp": chip * 2 + (1 - core)}
     peer = {"tp": (1 - chip) * 2 + core}
     R = x_own.shape[0]
+    S = 4 * R
+    xn[S:, :] = jnp.zeros_like(xn[S:, :])
+    h[S:, :] = jnp.zeros_like(h[S:, :])
     mine = core * 2 + chip
     across = core * 2 + (1 - chip)
 
@@ -50,12 +54,12 @@
             cols = pl.ds(j * BW1, BW1)
             loads1[l, j] = pltpu.make_async_copy(
                 w_in.at[l, :, cols], wv.at[2 * l, :, cols], wsem1.at[l, j])
-            loads1[l, j].start()
+            loads1[l, j].start(priority=1)
         for j in range(n2):
             cols = pl.ds(j * BW2, BW2)
             loads2[l, j] = pltpu.make_async_copy(
                 w_out.at[l, :, cols], wv.at[2 * l + 1, :, cols], wsem2.at[l, j])
-            loads2[l, j].start()
+            loads2[l, j].start(priority=1)
 
     barrier = pltpu.get_barrier_semaphore()
     for other in (mate, peer):
@@ -73,12 +77,14 @@
         copy.start()
         sends.append(copy)
 
-    load_x.wait()
-    load_g.wait()
+    with jax.named_scope('wait_x'):
+        load_x.wait()
+        load_g.wait()
     own = normalize(x_own[...].astype(jnp.float32), gam[0:1, :])
     for g in range(ng):
         xg[g, rows(mine), :] = own[:, g * GW:(g + 1) * GW]
-    pl.semaphore_wait(barrier, 2)
+    with jax.named_scope('barrier'):
+        pl.semaphore_wait(barrier, 2)
 
     arrive = {}
     for g in range(ng):
@@ -90,44 +96,51 @@
         arrive[g] = (to_peer, to_mate)
     relays = []
     for g in range(ng):
-        arrive[g][0].wait_recv()
+        with jax.named_scope(f'ag0_peer{g}'):
+            arrive[g][0].wait_recv()
         block = xg.at[g, rows(across)]
         relay = remote(block, block, g_sem, mate, 2, g)
         launch(relay)
         relays.append(relay)
     for g in range(ng):
-        arrive[g][1].wait_recv()
-        relays[g].wait_recv()
-        xn[:, g * GW:(g + 1) * GW] = xg[g]
+        with jax.named_scope(f'ag0_mate{g}'):
+            arrive[g][1].wait_recv()
+        with jax.named_scope(f'ag0_relay{g}'):
+            relays[g].wait_recv()
+        xn[0:S, g * GW:(g + 1) * GW] = xg[g]
 
     for l in range(n_layers):
         last = l == n_layers - 1
         for j in range(n1):
             cols = pl.ds(j * BW1, BW1)
-            loads1[l, j].wait()
-            u = jnp.dot(xn[...], wv[2 * l, :, cols], preferred_element_type=jnp.float32)
-            h[:, cols] = jax.nn.gelu(u, approximate=True).astype(jnp.bfloat16)
+            with jax.named_scope(f'w1_{l}_{j}'):
+                loads1[l, j].wait()
+            u = jnp.dot(xn[...], wv[2 * l, :, cols], preferred_element_type=jnp.float32)[:S]
+            h[0:S, cols] = jax.nn.gelu(u, approximate=True).astype(jnp.bfloat16)
 
         d2d, ici, yq, ym, yr = {}, {}, {}, {}, {}
         for step in range(n2 + max(LAG_SUM[l], LAG_OUT[l], LAG_RELAY[l])):
             j = step
             if j < n2:
                 cols = pl.ds(j * BW2, BW2)
-                loads2[l, j].wait()
-                part[l, j] = jnp.dot(h[...], wv[2 * l + 1, :, cols], preferred_element_type=jnp.float32)
+                with jax.named_scope(f'w2_{l}_{j}'):
+                    loads2[l, j].wait()
+                part[l, j] = jnp.dot(h[...], wv[2 * l + 1, :, cols], preferred_element_type=jnp.float32)[:S]
                 d2d[j] = remote(part.at[l, j, rows((1 - core) * 2, 2)], part_in.at[l, j],
                                 d2d_sem, mate, l, j)
                 launch(d2d[j])
             j = step - LAG_SUM[l]
             if 0 <= j < n2:
-                d2d[j].wait_recv()
+                with jax.named_scope(f'd2d_{l}_{j}'):
+                    d2d[j].wait_recv()
                 sum_out[l, j] = part[l, j, rows(across), :] + part_in[l, j, rows(1 - chip), :]
                 ici[j] = remote(sum_out.at[l, j], sum_in.at[l, j], ici_sem, peer, l, j)
                 launch(ici[j])
             j = step - LAG_OUT[l]
             if 0 <= j < n2:
                 cols = pl.ds(j * BW2, BW2)
-                ici[j].wait_recv()
+                with jax.named_scope(f'ici_{l}_{j}'):
+                    ici[j].wait_recv()
                 total = part[l, j, rows(mine), :] + part_in[l, j, rows(chip), :] + sum_in[l, j]
                 y = (x_own[:, cols].astype(jnp.float32) + total).astype(jnp.bfloat16)
                 if last:
@@ -142,21 +155,25 @@
                     launch(ym[j])
             j = step - LAG_RELAY[l]
             if not last and 0 <= j < n2:
-                yq[j].wait_recv()
+                with jax.named_scope(f'yq_{l}_{j}'):
+                    yq[j].wait_recv()
                 block = yg.at[j, rows(across)]
                 yr[j] = remote(block, block, y_sem, mate, 2, j)
                 launch(yr[j])
         if not last:
             for j in range(n2):
-                ym[j].wait_recv()
-                yr[j].wait_recv()
+                with jax.named_scope(f'ym_{l}_{j}'):
+                    ym[j].wait_recv()
+                with jax.named_scope(f'yr_{l}_{j}'):
+                    yr[j].wait_recv()
             for b in range(4):
                 r = slice(b * R, (b + 1) * R)
                 full = jnp.concatenate([yg[j, r, :] for j in range(n2)], axis=1)
                 xn[r, :] = normalize(full.astype(jnp.float32), gam[l + 1:l + 2, :])
 
-    for copy in sends:
-        copy.wait_send()
+    with jax.named_scope('drain'):
+        for copy in sends:
+            copy.wait_send()
 
 
 def solution(mesh):
@@ -176,8 +193,8 @@
                 pltpu.VMEM((R, width), bf16),
                 pltpu.VMEM((n_layers, width), f32),
                 pltpu.VMEM((ng, S, GW), bf16),
-                pltpu.VMEM((S, width), bf16),
-                pltpu.VMEM((S, ff), bf16),
+                pltpu.VMEM((MXU_ROWS, width), bf16),
+                pltpu.VMEM((MXU_ROWS, ff), bf16),
                 pltpu.VMEM((n_layers, n2, S, BW2), f32),
                 pltpu.VMEM((n_layers, n2, 2 * R, BW2), f32),
                 pltpu.VMEM((n_layers, n2, R, BW2), f32),

time: 56.4 us -> 36.5 us (0.65)
  Pallas kernels: 54.8 us -> 34.8 us
    pallas_call x1, Pallas kernels: 54.8 us -> 34.8 us  [local_stack(): pl.pallas_call(kernel, out_shape=jax.ShapeDtypeStruct((R, width), bf16),...]
where the time goes in v2:
time: 36.5 us; the launch traced here: 36.3 us
  Pallas kernels  34.8 us (95%)
  local copies, waits for them, and re-layouts  1.53 us (4%)
    pallas_call x1, Pallas kernels, local_stack(): pl.pallas_call(kernel, out_shape=jax.ShapeDtypeStruct((R, width), bf16),...  34.8 us
    unnamed x1, local copies, waits for them, and re-layouts  1.53 us

profile of v2, /device:TPU:0, one launch (start us, length us, event | category | flops | bytes accessed | tf_op | source)
XLA Modules:
  0.0 36.3 jit_solution(5076956343549497769)
XLA Ops:
  0.0 34.8 %mlp_stack.1 = bf16[16,2560]{1,0:T(8,128)(2,1)} custom-call(bf16[16,2560]{1,0:T(8,128)(2,1)} %x_hbm.1, f32[2,2560]{1,0:T(2,128)} %gam_hbm.1, bf16[2,2560,2560]{2,1,0:T(8,128)(2,1)} %w_in.1, bf16[2,2560,2560]{2,1,0:T(8,128)(2,1)} %w_out.1), custom_call_target="tpu_custom_call" | custom-call | tf_op jit(solution)/shard_map/mlp_stack/pallas_call | solution.py:186
  34.8 1.5 %copy.6 = bf16[16,2560]{1,0:T(8,128)(2,1)} copy(bf16[16,2560]{1,0:T(8,128)(2,1)} %mlp_stack.1) | data formatting | bytes 163840
